TPU v7x, 32 devices: a whole 2x2x4 slice. The times are simulated.
32 devices in a mesh: seq: 8 (over y, x, core), batch: 4 (over z).
Axes of the slice: x: 2, y: 2, z: 4, core: 2. Of those that a mesh axis runs over, the one named last changes fastest.
Arguments:
- queries: bfloat16 [4096, 4096], P(('batch', 'seq')), parts along dimension 0, may hold values from -6 to 6
- key_vectors: bfloat16 [4096, 4096], P(('batch', 'seq')), parts along dimension 0, may hold values from -6 to 6
- value_vectors: bfloat16 [4096, 4096], P(('batch', 'seq')), parts along dimension 0, may hold values from -6 to 6
- residual_in: bfloat16 [4096, 4096], P(('batch', 'seq')), parts along dimension 0, may hold values from -6 to 6
- input_logit: float32 [8, 4096], P(None, ('batch', 'seq')), parts along dimension 1, may hold values from -8 to 300
- forget_logit: float32 [8, 4096], P(None, ('batch', 'seq')), parts along dimension 1, may hold values from -3 to 13
- mix_gain: float32 [4096], replicated, may hold values from 0.1 to 1.9
- ffn_gain: float32 [4096], replicated, may hold values from 0.1 to 1.9
- expert_gate: bfloat16 [8, 4096, 704], P('seq'), may hold values from -0.09375 to 0.09375
- expert_up: bfloat16 [8, 4096, 704], P('seq'), may hold values from -0.09375 to 0.09375
- expert_down: bfloat16 [8, 704, 4096], P('seq'), may hold values from -0.21875 to 0.21875
- routes: int32 [4096, 2], P(('batch', 'seq')), parts along dimension 0, may hold values from 0 to 7, all different within a row; in each aligned block of 128 rows (0 to 127, 128 to 255, ...) at most 64 rows name the same one
- route_weight: float32 [4096, 2], P(('batch', 'seq')), parts along dimension 0, may hold values from 0.2 to 1
Outputs:
- block_out: bfloat16 [4096, 4096], P(('batch', 'seq')), parts along dimension 0
There are 4 independent parts, one for each index of `batch`. A program takes and returns all parts, laid end to end along the dimension named above; an argument that names none is the same for every part. Nothing has to cross between parts.
Inputs may be any that keep to these rules, and one draw needn't show every extreme that they name: `routes`: each row names two different experts. Within the rows of one device no expert is named by more than 64 rows, and in some device one expert is named by exactly 64 rows.
All inputs are finite; a program needn't handle non-finite values.
Results may differ from a plain program's by a relative error of at most 0.0081.
Values may be sent and summed in bfloat16 or wider, within the bound.
No kernel may reach another device: no remote copies, remote signals or barrier semaphores. Data moves between devices by JAX's collectives and lax.ppermute only.
A program may use at most 128 MiB of HBM per device.

v0:
```python
import math
import jax
import jax.numpy as jnp
from jax import lax
from jax.sharding import PartitionSpec as P

NEG_FILL = -1e30
EPSILON = 1e-06


def join_states(earlier, later):
    total_early, state_early, normv_early, peak_early = earlier
    total_late, state_late, normv_late, peak_late = later
    carried = total_late + peak_early
    peak_new = jnp.maximum(carried, peak_late)
    scale_early = jnp.exp(carried - peak_new)
    scale_late = jnp.exp(peak_late - peak_new)
    state_new = scale_early[..., None] * state_early + scale_late[..., None] * state_late
    normv_new = scale_early * normv_early + scale_late * normv_late
    return (total_early + total_late, state_new, normv_new, peak_new)


def block_state(keys_three, values_three, log_forget, input_gate):
    cumul_log = jnp.cumsum(log_forget, axis=1)
    tail_log = cumul_log[:, -1:] - cumul_log + input_gate
    peak_tail = jnp.max(tail_log, axis=1)
    weight = jnp.exp(tail_log - peak_tail[:, None])
    weighted = keys_three.astype(jnp.float32) * jnp.transpose(weight)[:, :, None]
    rounded = weighted.astype(jnp.bfloat16)
    state_mat = jnp.einsum(
        "thd,the->hde", rounded, values_three, preferred_element_type=jnp.float32
    )
    norm_vec = jnp.sum(weighted, axis=0)
    return (
        jnp.broadcast_to(cumul_log[:, -1:], norm_vec.shape),
        state_mat,
        norm_vec,
        jnp.broadcast_to(peak_tail[:, None], norm_vec.shape),
    )


def block_mix(queries_three, keys_three, values_three, log_forget, input_gate, carry_in):
    tokens = queries_three.shape[0]
    inverse_root = 1.0 / math.sqrt(queries_three.shape[2])
    cumul_log = jnp.cumsum(log_forget, axis=1)
    carry_total, carry_state, carry_norm, carry_peak = carry_in
    log_weight = cumul_log[:, :, None] - cumul_log[:, None, :] + input_gate[:, None, :]
    causal = jnp.arange(tokens)[:, None] >= jnp.arange(tokens)[None, :]
    log_weight = jnp.where(causal[None], log_weight, NEG_FILL)
    carried = cumul_log + carry_peak[:, 0:1]
    peak_log = jnp.maximum(jnp.max(log_weight, axis=2), carried)
    decay_mat = jnp.exp(log_weight - peak_log[:, :, None])
    scores = (
        jnp.einsum("thd,shd->hts", queries_three, keys_three, preferred_element_type=jnp.float32)
        * inverse_root
    )
    coef = decay_mat * scores
    denom_sum = jnp.sum(coef, axis=2)
    numer_sum = jnp.einsum(
        "hts,she->the", coef.astype(jnp.bfloat16), values_three, preferred_element_type=jnp.float32
    )
    carry_reach = jnp.exp(carried - peak_log) * inverse_root
    query_float = queries_three.astype(jnp.float32)
    from_state = jnp.einsum(
        "thd,hde->the", query_float, carry_state, precision=lax.Precision.HIGHEST
    )
    from_norm = jnp.einsum("thd,hd->ht", query_float, carry_norm, precision=lax.Precision.HIGHEST)
    numer_sum = numer_sum + jnp.transpose(carry_reach)[:, :, None] * from_state
    denom_sum = denom_sum + carry_reach * from_norm
    floor_sum = jnp.maximum(jnp.abs(denom_sum), 1.0)
    return numer_sum / jnp.transpose(floor_sum)[:, :, None]


def shards(
    queries,
    key_vectors,
    value_vectors,
    residual_in,
    input_logit,
    forget_logit,
    mix_gain,
    ffn_gain,
    expert_gate,
    expert_up,
    expert_down,
    routes,
    route_weight,
):
    tokens, model_width = queries.shape
    head_count = input_logit.shape[0]
    head_dim = model_width // head_count
    devices = lax.axis_size("seq")
    queries_three = queries.reshape(tokens, head_count, head_dim)
    keys_three = key_vectors.reshape(tokens, head_count, head_dim)
    group = devices // head_count
    group_width = model_width // devices
    query_send = jnp.repeat(queries_three, group, axis=1)
    key_send = jnp.repeat(keys_three, group, axis=1)
    value_send = value_vectors.reshape(tokens, devices, group_width)
    query_all, key_all, value_all = (
        lax.all_to_all(query_send, "seq", split_axis=1, concat_axis=0, tiled=True),
        lax.all_to_all(key_send, "seq", split_axis=1, concat_axis=0, tiled=True),
        lax.all_to_all(value_send, "seq", split_axis=1, concat_axis=0, tiled=True),
    )
    input_all, forget_all = (
        lax.all_gather(input_logit, "seq", axis=1, tiled=True),
        lax.all_gather(forget_logit, "seq", axis=1, tiled=True),
    )
    head_index = lax.axis_index("seq") // group
    input_head = lax.dynamic_slice_in_dim(input_all, head_index, 1, 0)
    forget_head = jax.nn.log_sigmoid(lax.dynamic_slice_in_dim(forget_all, head_index, 1, 0))

    def per_block(array):
        return array.reshape((devices, tokens) + array.shape[1:])

    def per_gate(array):
        return jnp.transpose(array.reshape(1, devices, tokens), (1, 0, 2))

    start = (
        jnp.zeros((1, head_dim), jnp.float32),
        jnp.zeros((1, head_dim, group_width), jnp.float32),
        jnp.zeros((1, head_dim), jnp.float32),
        jnp.full((1, head_dim), NEG_FILL, jnp.float32),
    )

    def advance(carry_in, pieces):
        query_block, key_block, value_block, forget_block, input_block = pieces
        result = block_mix(query_block, key_block, value_block, forget_block, input_block, carry_in)
        carry_out = join_states(
            carry_in, block_state(key_block, value_block, forget_block, input_block)
        )
        return (carry_out, result)

    unused, mixed = lax.scan(
        advance,
        start,
        (
            per_block(query_all),
            per_block(key_all),
            per_block(value_all),
            per_gate(forget_head),
            per_gate(input_head),
        ),
    )
    mixed = mixed.reshape(devices * tokens, 1, group_width)
    mixer_out = lax.all_to_all(mixed, "seq", split_axis=0, concat_axis=1, tiled=True).reshape(
        tokens, model_width
    )
    mixer_square = jnp.mean(mixer_out * mixer_out, axis=1, keepdims=True)
    updated = (
        residual_in.astype(jnp.float32) + mixer_out * lax.rsqrt(mixer_square + EPSILON) * mix_gain
    ).astype(jnp.bfloat16)
    updated_float = updated.astype(jnp.float32)
    updated_square = jnp.mean(updated_float * updated_float, axis=1, keepdims=True)
    normed = (updated_float * lax.rsqrt(updated_square + EPSILON) * ffn_gain).astype(jnp.bfloat16)
    capacity = 4 * tokens // devices
    flat_routes = routes.reshape(-1)
    matches = (flat_routes[:, None] == jnp.arange(devices, dtype=jnp.int32)[None, :]).astype(
        jnp.int32
    )
    before = jnp.cumsum(matches, axis=0) - matches
    position = jnp.sum(before * matches, axis=1)
    slot_index = (flat_routes * capacity + position).reshape(tokens, 2)
    columns = jnp.arange(devices * capacity, dtype=jnp.int32)
    pick_first = (slot_index[:, 0:1] == columns[None, :]).astype(jnp.bfloat16)
    pick_second = (slot_index[:, 1:2] == columns[None, :]).astype(jnp.bfloat16)
    spread = jnp.einsum(
        "tc,td->cd", pick_first + pick_second, normed, preferred_element_type=jnp.float32
    ).astype(jnp.bfloat16)
    outbound = spread.reshape(devices, capacity, model_width)
    block_in = lax.all_to_all(outbound, "seq", split_axis=0, concat_axis=0, tiled=True)
    row_block = block_in.reshape(-1, model_width)
    gate_val = jnp.dot(row_block, expert_gate[0], preferred_element_type=jnp.float32)
    up_val = jnp.dot(row_block, expert_up[0], preferred_element_type=jnp.float32)
    hidden = (jax.nn.silu(gate_val) * up_val).astype(jnp.bfloat16)
    result = jnp.dot(hidden, expert_down[0], preferred_element_type=jnp.float32).astype(
        jnp.bfloat16
    )
    inbound = lax.all_to_all(
        result.reshape(block_in.shape), "seq", split_axis=0, concat_axis=0, tiled=True
    )
    flat_back = inbound.reshape(devices * capacity, model_width)
    first_out = jnp.dot(pick_first, flat_back, preferred_element_type=jnp.float32)
    second_out = jnp.dot(pick_second, flat_back, preferred_element_type=jnp.float32)
    expert_mix = route_weight[:, 0:1] * first_out + route_weight[:, 1:2] * second_out
    return (updated_float + expert_mix).astype(jnp.bfloat16)


def solution(mesh):
    return jax.shard_map(
        shards,
        mesh=mesh,
        in_specs=(
            P(("batch", "seq"), None),
            P(("batch", "seq"), None),
            P(("batch", "seq"), None),
            P(("batch", "seq"), None),
            P(None, ("batch", "seq")),
            P(None, ("batch", "seq")),
            P(),
            P(),
            P("seq", None, None),
            P("seq", None, None),
            P("seq", None, None),
            P(("batch", "seq"), None),
            P(("batch", "seq"), None),
        ),
        out_specs=P(("batch", "seq"), None),
        check_vma=False,
    )
```

profile of v0, /device:TPU:0, one launch (start us, length us, event | category | flops | bytes accessed | tf_op | source)
XLA Modules:
  0.0 361.2 jit_solution(481874486688636953)
XLA Ops:
  0.0 2.3 copy.82
  2.3 5.2 %all-to-all-start = ((bf16[128,8,512]{0,2,1:T(8,128)(2,1)}), bf16[128,8,512]{0,2,1:T(8,128)(2,1)S(1)}, u32[]{:S(2)}, u32[]{:S(2)}) async-start(bf16[128,8,512]{0,2,1:T(8,128)(2,1)} %bitcast.2), calls=%async_computation | async-start | bytes 2097152 | tf_op jit(solution)/shard_map/all_to_all | solution.py:102
  7.6 1.3 copy.84
  8.9 14.1 %all-to-all-done = bf16[128,8,512]{0,2,1:T(8,128)(2,1)S(1)} async-done(((bf16[128,8,512]{0,2,1:T(8,128)(2,1)}), bf16[128,8,512]{0,2,1:T(8,128)(2,1)S(1)}, u32[]{:S(2)}, u32[]{:S(2)}) %all-to-all-start) | async-done | bytes 1048608 | tf_op jit(solution)/shard_map/all_to_all | solution.py:102
  22.9 3.6 all-to-all-start.1
  26.5 1.3 copy.86
  27.8 14.0 %all-to-all-done.1 = bf16[128,8,512]{0,2,1:T(8,128)(2,1)S(1)} async-done(((bf16[128,8,512]{0,2,1:T(8,128)(2,1)}), bf16[128,8,512]{0,2,1:T(8,128)(2,1)S(1)}, u32[]{:S(2)}, u32[]{:S(2)}) %all-to-all-start.1) | async-done | bytes 1048608 | tf_op jit(solution)/shard_map/all_to_all | solution.py:103
  41.8 4.2 %all-to-all-start.2 = ((bf16[128,8,512]{0,2,1:T(8,128)(2,1)}), bf16[128,8,512]{0,2,1:T(8,128)(2,1)}, u32[]{:S(2)}, u32[]{:S(2)}) async-start(bf16[128,8,512]{0,2,1:T(8,128)(2,1)} %bitcast.8), calls=%async_computation.2 | async-start | bytes 2097152 | tf_op jit(solution)/shard_map/all_to_all | solution.py:101
  46.1 18.5 %all_gather.7 = f32[8,1024]{1,0:T(8,128)S(1)} all-gather(f32[8,128]{1,0:T(8,128)S(1)} %copy-done.9), channel_id=1, replica_groups=mesh['seq'=8,'batch'=4] {'seq'}, dimensions={1}, use_global_device_ids=true | all-gather | bytes 36864 | tf_op jit(solution)/shard_map/all_gather | solution.py:106
  64.6 8.2 %all_gather.6 = f32[8,1024]{1,0:T(8,128)S(1)} all-gather(f32[8,128]{1,0:T(8,128)S(1)} %copy-done.10), channel_id=1, replica_groups=mesh['seq'=8,'batch'=4] {'seq'}, dimensions={1}, use_global_device_ids=true | all-gather | bytes 36864 | tf_op jit(solution)/shard_map/all_gather | solution.py:107
  72.8 1.7 copy.83
  74.5 1.5 copy.88
  76.1 1.7 copy.85
  77.8 1.5 copy.89
  79.3 2.7 copy.87
  82.0 2.5 copy.90
  84.5 105.7 %while.17 = (s32[]{:T(128)}, f32[1,512,512]{2,1,0:T(8,128)S(1)}, f32[1,512]{1,0:T(1,128)S(1)}, f32[1,512]{1,0:T(1,128)S(1)}, f32[8,128,1,512]{3,1,0,2:T(8,128)},...) while((s32[]{:T(128)}, f32[1,512,512]{2,1,0:T(8,128)S(1)}, ...), condition=%wide.region_6.7_spmd.clone, body=%wide.region_0.6_spmd.clone.sunk | while | flops 506255232 | bytes 14530822 | solution.py:134
  85.5 1.3 fusion.115
  86.8 1.3 subtract_exponential_fusion.6
  88.1 1.3 multiply_add_fusion.3
  93.3 2.0 fusion.120
  96.1 1.5 fusion.117
  98.7 1.3 fusion.115
  100.0 1.3 subtract_exponential_fusion.6
  101.3 1.3 multiply_add_fusion.3
  106.5 2.0 fusion.120
  109.3 1.5 fusion.117
  111.9 1.3 fusion.115
  114.6 1.3 multiply_add_fusion.3
  119.7 2.0 fusion.120
  122.5 1.5 fusion.117
  125.1 1.3 fusion.115
  127.8 1.3 multiply_add_fusion.3
  132.9 2.0 fusion.120
  135.8 1.5 fusion.117
  138.3 1.3 fusion.115
  139.6 1.3 subtract_exponential_fusion.6
  141.0 1.3 multiply_add_fusion.3
  146.1 2.0 fusion.120
  149.0 1.5 fusion.117
  151.5 1.3 fusion.115
  154.2 1.3 multiply_add_fusion.3
  159.4 2.0 fusion.120
  162.2 1.5 fusion.117
  164.8 1.3 fusion.115
  167.4 1.3 multiply_add_fusion.3
  172.6 2.0 fusion.120
  175.5 1.5 fusion.117
  178.0 1.3 fusion.115
  180.7 1.3 multiply_add_fusion.3
  185.8 2.0 fusion.120
  188.7 1.5 fusion.117
  190.2 5.0 %copy.92 = f32[1024,1,512]{2,1,0:T(1,128)} copy(f32[1024,1,512]{2,0,1:T(8,128)} %bitcast.226) | data formatting | bytes 4194304 | tf_op jit(solution)/shard_map/reshape | solution.py:145
  195.2 3.9 %all-to-all-start.3 = ((f32[1024,1,512]{2,1,0:T(1,128)}), f32[1024,1,512]{2,1,0:T(1,128)S(1)}, u32[]{:S(2)}, u32[]{:S(2)}) async-start(f32[1024,1,512]{2,1,0:T(1,128)} %copy.92), calls=%async_computation.3 | async-start | bytes 4194304 | tf_op jit(solution)/shard_map/all_to_all | solution.py:146
  200.7 24.8 %all-to-all-done.3 = f32[1024,1,512]{2,1,0:T(1,128)S(1)} async-done(((f32[1024,1,512]{2,1,0:T(1,128)}), f32[1024,1,512]{2,1,0:T(1,128)S(1)}, u32[]{:S(2)}, u32[]{:S(2)}) %all-to-all-start.3) | async-done | bytes 2097184 | tf_op jit(solution)/shard_map/all_to_all | solution.py:146
  227.9 1.4 convolution_convert_fusion
  229.3 51.7 %all_to_all.70 = bf16[8,64,4096]{2,1,0:T(8,128)(2,1)S(1)} all-to-all(bf16[8,64,4096]{2,1,0:T(8,128)(2,1)S(1)} %bitcast.216), channel_id=1, replica_groups=mesh['seq'=8,'batch'=4] {'seq'}, dimensions={0} | all-to-all | bytes 8388608 | tf_op jit(solution)/shard_map/all_to_all | solution.py:171
  281.0 2.0 copy-done.2
  282.9 3.2 fusion.50
  286.1 14.1 %convolution_convert_fusion.1 = bf16[512,4096]{1,0:T(8,128)(2,1)} fusion(bf16[1,704,4096]{2,1,0:T(8,128)(2,1)} %param.25, bf16[512,4096]{1,0:T(8,128)(2,1)} %bitcast.222, bf16[1,4096,704]{1,2,0:T(8,128)(2,1)} %param.24, f32[512,704]{0,1:T(8,128)S(1)} %fusion.50), kind=kOutput, calls=%fused_computation.70 | convolution fusion | flops 5909839872 | bytes 21364736 | tf_op jit(solution)/shard_map/dot_general | solution.py:176
  300.2 4.7 %all-to-all-start.5 = ((bf16[8,64,4096]{2,1,0:T(8,128)(2,1)}), bf16[8,64,4096]{2,1,0:T(8,128)(2,1)}, u32[]{:S(2)}, u32[]{:S(2)}) async-start(bf16[8,64,4096]{2,1,0:T(8,128)(2,1)} %bitcast.220), calls=%async_computation.5 | async-start | bytes 8388608 | tf_op jit(solution)/shard_map/all_to_all | solution.py:179
  304.9 49.1 %all-to-all-done.5 = bf16[8,64,4096]{2,1,0:T(8,128)(2,1)} async-done(((bf16[8,64,4096]{2,1,0:T(8,128)(2,1)}), bf16[8,64,4096]{2,1,0:T(8,128)(2,1)}, u32[]{:S(2)}, u32[]{:S(2)}) %all-to-all-start.5) | async-done | bytes 4194336 | tf_op jit(solution)/shard_map/all_to_all | solution.py:179
  354.0 2.9 convolution_multiply_fusion.3
  356.9 4.2 %fusion.54 = bf16[128,4096]{1,0:T(8,128)(2,1)} fusion(f32[128,4096]{1,0:T(8,128)S(1)} %convolution_multiply_fusion.3, bf16[512,4096]{1,0:T(8,128)(2,1)} %bitcast.24, bf16[128,4096]{1,0:T(8,128)(2,1)S(1)} %get-tuple-element.169, f32[128]{0:T(128)S(1)} %get-tuple-element.174, s32[128]{0:T(128)S(1)} %get-tuple-element.177), kind=kOutput, calls=%fused_computation.80 | convolution fusion | flops 539557888 | bytes 8389632 | tf_op jit(solution)/shard_map/dot_general | solution.py:184
  (192 shorter events, 56.8 us)
Async XLA Ops:
  0.0 7.6 %copy-start.4 = (bf16[128,4096]{1,0:T(8,128)(2,1)S(1)}, bf16[128,4096]{1,0:T(8,128)(2,1)}, u32[]{:S(2)}) copy-start(bf16[128,4096]{1,0:T(8,128)(2,1)} %param.17) | copy-start | bytes 3145732
  2.3 20.6 %all-to-all-start = ((bf16[128,8,512]{0,2,1:T(8,128)(2,1)}), bf16[128,8,512]{0,2,1:T(8,128)(2,1)S(1)}, u32[]{:S(2)}, u32[]{:S(2)}) async-start(bf16[128,8,512]{0,2,1:T(8,128)(2,1)} %bitcast.2), calls=%async_computation | async-start | bytes 2097152 | tf_op jit(solution)/shard_map/all_to_all | solution.py:102
  8.9 17.6 %copy-start.5 = (bf16[128,4096]{1,0:T(8,128)(2,1)S(1)}, bf16[128,4096]{1,0:T(8,128)(2,1)}, u32[]{:S(2)}) copy-start(bf16[128,4096]{1,0:T(8,128)(2,1)} %param.15) | copy-start | bytes 3145732
  22.9 18.9 %all-to-all-start.1 = ((bf16[128,8,512]{0,2,1:T(8,128)(2,1)}), bf16[128,8,512]{0,2,1:T(8,128)(2,1)S(1)}, u32[]{:S(2)}, u32[]{:S(2)}) async-start(bf16[128,8,512]{0,2,1:T(8,128)(2,1)} %bitcast.5), calls=%async_computation.1 | async-start | bytes 2097152 | tf_op jit(solution)/shard_map/all_to_all | solution.py:103
  26.5 19.6 %copy-start.9 = (f32[8,128]{1,0:T(8,128)S(1)}, f32[8,128]{1,0:T(8,128)}, u32[]{:S(2)}) copy-start(f32[8,128]{1,0:T(8,128)} %param.19) | copy-start | bytes 12292
  26.5 38.1 %copy-start.10 = (f32[8,128]{1,0:T(8,128)S(1)}, f32[8,128]{1,0:T(8,128)}, u32[]{:S(2)}) copy-start(f32[8,128]{1,0:T(8,128)} %param.20) | copy-start | bytes 12292
  41.8 37.5 %all-to-all-start.2 = ((bf16[128,8,512]{0,2,1:T(8,128)(2,1)}), bf16[128,8,512]{0,2,1:T(8,128)(2,1)}, u32[]{:S(2)}, u32[]{:S(2)}) async-start(bf16[128,8,512]{0,2,1:T(8,128)(2,1)} %bitcast.8), calls=%async_computation.2 | async-start | bytes 2097152 | tf_op jit(solution)/shard_map/all_to_all | solution.py:101
  84.5 8.8 %copy-start = (bf16[8,128,1,512]{3,1,2,0:T(8,128)(2,1)}, bf16[8,128,1,512]{3,1,2,0:T(8,128)(2,1)S(1)}, u32[]{:S(2)}) copy-start(bf16[8,128,1,512]{3,1,2,0:T(8,128)(2,1)S(1)} %get-tuple-element.297) | copy-start | bytes 3145732 | tf_op jit(solution)/shard_map/while
  96.1 1.5 copy-start.1
  97.7 8.8 %copy-start = (bf16[8,128,1,512]{3,1,2,0:T(8,128)(2,1)}, bf16[8,128,1,512]{3,1,2,0:T(8,128)(2,1)S(1)}, u32[]{:S(2)}) copy-start(bf16[8,128,1,512]{3,1,2,0:T(8,128)(2,1)S(1)} %get-tuple-element.297) | copy-start | bytes 3145732 | tf_op jit(solution)/shard_map/while
  109.3 1.5 copy-start.1
  110.9 8.8 %copy-start = (bf16[8,128,1,512]{3,1,2,0:T(8,128)(2,1)}, bf16[8,128,1,512]{3,1,2,0:T(8,128)(2,1)S(1)}, u32[]{:S(2)}) copy-start(bf16[8,128,1,512]{3,1,2,0:T(8,128)(2,1)S(1)} %get-tuple-element.297) | copy-start | bytes 3145732 | tf_op jit(solution)/shard_map/while
  122.5 1.5 copy-start.1
  124.1 8.8 %copy-start = (bf16[8,128,1,512]{3,1,2,0:T(8,128)(2,1)}, bf16[8,128,1,512]{3,1,2,0:T(8,128)(2,1)S(1)}, u32[]{:S(2)}) copy-start(bf16[8,128,1,512]{3,1,2,0:T(8,128)(2,1)S(1)} %get-tuple-element.297) | copy-start | bytes 3145732 | tf_op jit(solution)/shard_map/while
  135.8 1.5 copy-start.1
  137.3 8.9 %copy-start = (bf16[8,128,1,512]{3,1,2,0:T(8,128)(2,1)}, bf16[8,128,1,512]{3,1,2,0:T(8,128)(2,1)S(1)}, u32[]{:S(2)}) copy-start(bf16[8,128,1,512]{3,1,2,0:T(8,128)(2,1)S(1)} %get-tuple-element.297) | copy-start | bytes 3145732 | tf_op jit(solution)/shard_map/while
  149.0 1.5 copy-start.1
  150.5 8.8 %copy-start = (bf16[8,128,1,512]{3,1,2,0:T(8,128)(2,1)}, bf16[8,128,1,512]{3,1,2,0:T(8,128)(2,1)S(1)}, u32[]{:S(2)}) copy-start(bf16[8,128,1,512]{3,1,2,0:T(8,128)(2,1)S(1)} %get-tuple-element.297) | copy-start | bytes 3145732 | tf_op jit(solution)/shard_map/while
  162.2 1.5 copy-start.1
  163.8 8.8 %copy-start = (bf16[8,128,1,512]{3,1,2,0:T(8,128)(2,1)}, bf16[8,128,1,512]{3,1,2,0:T(8,128)(2,1)S(1)}, u32[]{:S(2)}) copy-start(bf16[8,128,1,512]{3,1,2,0:T(8,128)(2,1)S(1)} %get-tuple-element.297) | copy-start | bytes 3145732 | tf_op jit(solution)/shard_map/while
  175.4 1.5 copy-start.1
  177.0 8.8 %copy-start = (bf16[8,128,1,512]{3,1,2,0:T(8,128)(2,1)}, bf16[8,128,1,512]{3,1,2,0:T(8,128)(2,1)S(1)}, u32[]{:S(2)}) copy-start(bf16[8,128,1,512]{3,1,2,0:T(8,128)(2,1)S(1)} %get-tuple-element.297) | copy-start | bytes 3145732 | tf_op jit(solution)/shard_map/while
  188.7 1.5 copy-start.1
  195.2 3.9 %copy-start.8 = (s32[128,2]{0,1:T(2,128)S(1)}, s32[128,2]{0,1:T(2,128)}, u32[]{:S(2)}) copy-start(s32[128,2]{0,1:T(2,128)} %param.26) | copy-start | bytes 3076
  195.2 30.3 %all-to-all-start.3 = ((f32[1024,1,512]{2,1,0:T(1,128)}), f32[1024,1,512]{2,1,0:T(1,128)S(1)}, u32[]{:S(2)}, u32[]{:S(2)}) async-start(f32[1024,1,512]{2,1,0:T(1,128)} %copy.92), calls=%async_computation.3 | async-start | bytes 4194304 | tf_op jit(solution)/shard_map/all_to_all | solution.py:146
  225.9 1.2 copy-start.3
  226.0 1.2 copy-start.6
  227.2 0.7 copy-start.7
  227.9 55.0 %slice-start = ((s8[5767168]{0:T(1024)(128)(4,1)}), s8[4194304]{0:T(1024)(128)(4,1)S(1)}, s32[]{:S(2)}) async-start(s8[5767168]{0:T(1024)(128)(4,1)} %bitcast.232), calls=%async_computation.6 | async-start | bytes 8388608
  229.3 53.6 %slice-start.1 = ((s8[5767168]{0:T(1024)(128)(4,1)}), s8[1572864]{0:T(1024)(128)(4,1)S(1)}, s32[]{:S(2)}) async-start(s8[5767168]{0:T(1024)(128)(4,1)} %bitcast.232), calls=%async_computation.7 | async-start | bytes 3145728
  281.0 2.0 copy-start.2
  300.2 4.7 %copy-start.11 = (f32[128,2]{0,1:T(2,128)S(1)}, f32[128,2]{0,1:T(2,128)}, u32[]{:S(2)}) copy-start(f32[128,2]{0,1:T(2,128)} %param.27) | copy-start | bytes 3076
  300.2 53.8 %all-to-all-start.5 = ((bf16[8,64,4096]{2,1,0:T(8,128)(2,1)}), bf16[8,64,4096]{2,1,0:T(8,128)(2,1)}, u32[]{:S(2)}, u32[]{:S(2)}) async-start(bf16[8,64,4096]{2,1,0:T(8,128)(2,1)} %bitcast.220), calls=%async_computation.5 | async-start | bytes 8388608 | tf_op jit(solution)/shard_map/all_to_all | solution.py:179
where the time goes:
time: 363 us; the launch traced here: 361 us
  waiting for transfers between devices  102 us (28%)
  blocking collectives  78.4 us (22%)
  matrix products  72.6 us (20%)
  local copies, waits for them, and re-layouts  42.9 us (12%)
  other arithmetic  42.8 us (12%)
  starting transfers between devices  21.6 us (6%)
    all_to_all x1, blocking collectives, shards(): lax.all_to_all(outbound, 'seq', split_axis=0, concat_axis=0, tiled=True)  51.7 us
    all_to_all x1, waiting for transfers between devices, shards(): lax.all_to_all(result.reshape(block_in.shape), 'seq', split_axis=0, conca...  49.1 us
    all_to_all x1, waiting for transfers between devices, shards(): lax.all_to_all(mixed, 'seq', split_axis=0, concat_axis=1, tiled=True)  24.8 us
    all_gather x1, blocking collectives, shards(): lax.all_gather(input_logit, 'seq', axis=1, tiled=True)  18.5 us
    dot_general x8, matrix products, block_mix(): jnp.einsum('thd,hde->the', query_float, carry_state, precision=lax.Precis...  15.8 us
    dot_general x1, matrix products, shards(): jnp.dot(hidden, expert_down[0], preferred_element_type=jnp.float32)  14.1 us
    unnamed x33, local copies, waits for them, and re-layouts  14.1 us
    all_to_all x1, waiting for transfers between devices, shards(): lax.all_to_all(key_send, 'seq', split_axis=1, concat_axis=0, tiled=True)  14.1 us
  transfers between devices with their start and end apart: 5, of which 4 were waited for; matrix products, arithmetic and copies ran while one was open for 3% of the time, Pallas kernels for 0%

commit v1 on v0

--- a/solution.py
+++ b/solution.py
@@ -86,6 +86,22 @@
     routes,
     route_weight,
 ):
+
+    def plan_matrix(in_array):
+        high, h_now = (lax.axis_size("seq"), lax.axis_index("seq"))
+        inter = in_array.shape[0] // high
+        small = jnp.roll(in_array, shift=-h_now * inter, axis=0)
+        store = [lax.slice_in_dim(small, 0, inter, axis=0)]
+        for jj in [*range(1, high)]:
+            newest = lax.slice_in_dim(small, jj * inter, (jj + 1) * inter, axis=0)
+            store.append(
+                lax.ppermute(newest, "seq", [(dev_i, (dev_i + jj) % high) for dev_i in range(high)])
+            )
+        after = jnp.roll(
+            jnp.concatenate(store[::-1], axis=0), shift=(h_now + 1) * store[0].shape[0], axis=0
+        )
+        return after
+
     tokens, model_width = queries.shape
     head_count = input_logit.shape[0]
     head_dim = model_width // head_count
@@ -168,7 +184,7 @@
         "tc,td->cd", pick_first + pick_second, normed, preferred_element_type=jnp.float32
     ).astype(jnp.bfloat16)
     outbound = spread.reshape(devices, capacity, model_width)
-    block_in = lax.all_to_all(outbound, "seq", split_axis=0, concat_axis=0, tiled=True)
+    block_in = plan_matrix(outbound)
     row_block = block_in.reshape(-1, model_width)
     gate_val = jnp.dot(row_block, expert_gate[0], preferred_element_type=jnp.float32)
     up_val = jnp.dot(row_block, expert_up[0], preferred_element_type=jnp.float32)

time: 363 us -> 369 us (1.017)
  blocking collectives: 78.4 us -> 26.7 us
  waiting for transfers between devices: 102 us -> 144 us
  matrix products: 72.6 us -> 79 us
  local copies, waits for them, and re-layouts: 42.9 us -> 48 us
    all_to_all x1 -> x0, blocking collectives: 51.7 us -> none  [shards(): lax.all_to_all(outbound, 'seq', split_axis=0, concat_axis=0, tiled=True)]
    ppermute x0 -> x7, waiting for transfers between devices: none -> 43.5 us  [plan_matrix(): lax.ppermute(newest, 'seq', [(dev_i, (dev_i + jj) % high) for dev_i in ra...]
    dot_general x8, matrix products: 1.7 us -> 8.9 us  [block_mix(): jnp.einsum('hts,she->the', coef.astype(jnp.bfloat16), values_three, prefe...]
    unnamed x33 -> x40, local copies, waits for them, and re-layouts: 14.1 us -> 18.8 us
  transfers between devices with their start and end apart: 5 -> 12, of which waited for: 4 -> 9; matrix products, arithmetic and copies ran while one was open for 3% -> 4% of each run, Pallas kernels for 0% -> 0%
where the time goes in v1:
time: 369 us; the launch traced here: 367 us
  waiting for transfers between devices  144 us (39%)
  matrix products  79 us (21%)
  local copies, waits for them, and re-layouts  48 us (13%)
  other arithmetic  42.9 us (12%)
  blocking collectives  26.7 us (7%)
  starting transfers between devices  24.9 us (7%)
    all_to_all x1, waiting for transfers between devices, shards(): lax.all_to_all(result.reshape(block_in.shape), 'seq', split_axis=0, conca...  49.1 us
    ppermute x7, waiting for transfers between devices, plan_matrix(): lax.ppermute(newest, 'seq', [(dev_i, (dev_i + jj) % high) for dev_i in ra...  43.5 us
    all_to_all x1, waiting for transfers between devices, shards(): lax.all_to_all(mixed, 'seq', split_axis=0, concat_axis=1, tiled=True)  24.7 us
    unnamed x40, local copies, waits for them, and re-layouts  18.8 us
    all_gather x1, blocking collectives, shards(): lax.all_gather(input_logit, 'seq', axis=1, tiled=True)  18.5 us
    dot_general x8, matrix products, block_mix(): jnp.einsum('thd,hde->the', query_float, carry_state, precision=lax.Precis...  15.8 us
    dot_general x1, matrix products, shards(): jnp.dot(hidden, expert_down[0], preferred_element_type=jnp.float32)  14.1 us
    all_to_all x1, waiting for transfers between devices, shards(): lax.all_to_all(key_send, 'seq', split_axis=1, concat_axis=0, tiled=True)  14 us
  transfers between devices with their start and end apart: 12, of which 9 were waited for; matrix products, arithmetic and copies ran while one was open for 4% of the time, Pallas kernels for 0%

profile of v1, /device:TPU:0, one launch (start us, length us, event | category | flops | bytes accessed | tf_op | source)
XLA Modules:
  0.0 367.0 jit_solution(16989798288383947038)
XLA Ops:
  0.0 2.3 copy.82
  2.3 5.2 %all-to-all-start = ((bf16[128,8,512]{0,2,1:T(8,128)(2,1)}), bf16[128,8,512]{0,2,1:T(8,128)(2,1)S(1)}, u32[]{:S(2)}, u32[]{:S(2)}) async-start(bf16[128,8,512]{0,2,1:T(8,128)(2,1)} %bitcast.2), calls=%async_computation | async-start | bytes 2097152 | tf_op jit(solution)/shard_map/all_to_all | solution.py:118
  7.6 1.3 copy.84
  8.9 14.0 %all-to-all-done = bf16[128,8,512]{0,2,1:T(8,128)(2,1)S(1)} async-done(((bf16[128,8,512]{0,2,1:T(8,128)(2,1)}), bf16[128,8,512]{0,2,1:T(8,128)(2,1)S(1)}, u32[]{:S(2)}, u32[]{:S(2)}) %all-to-all-start) | async-done | bytes 1048608 | tf_op jit(solution)/shard_map/all_to_all | solution.py:118
  22.9 3.6 all-to-all-start.1
  26.5 2.3 copy.86
  28.7 13.1 %all-to-all-done.1 = bf16[128,8,512]{0,2,1:T(8,128)(2,1)S(1)} async-done(((bf16[128,8,512]{0,2,1:T(8,128)(2,1)}), bf16[128,8,512]{0,2,1:T(8,128)(2,1)S(1)}, u32[]{:S(2)}, u32[]{:S(2)}) %all-to-all-start.1) | async-done | bytes 1048608 | tf_op jit(solution)/shard_map/all_to_all | solution.py:119
  41.8 4.2 %all-to-all-start.2 = ((bf16[128,8,512]{0,2,1:T(8,128)(2,1)}), bf16[128,8,512]{0,2,1:T(8,128)(2,1)}, u32[]{:S(2)}, u32[]{:S(2)}) async-start(bf16[128,8,512]{0,2,1:T(8,128)(2,1)} %bitcast.8), calls=%async_computation.2 | async-start | bytes 2097152 | tf_op jit(solution)/shard_map/all_to_all | solution.py:117
  46.1 18.5 %all_gather.7 = f32[8,1024]{1,0:T(8,128)S(1)} all-gather(f32[8,128]{1,0:T(8,128)S(1)} %copy-done.7), channel_id=1, replica_groups=mesh['seq'=8,'batch'=4] {'seq'}, dimensions={1}, use_global_device_ids=true | all-gather | bytes 36864 | tf_op jit(solution)/shard_map/all_gather | solution.py:122
  64.6 8.2 %all_gather.6 = f32[8,1024]{1,0:T(8,128)S(1)} all-gather(f32[8,128]{1,0:T(8,128)S(1)} %copy-done.8), channel_id=1, replica_groups=mesh['seq'=8,'batch'=4] {'seq'}, dimensions={1}, use_global_device_ids=true | all-gather | bytes 36864 | tf_op jit(solution)/shard_map/all_gather | solution.py:123
  72.8 1.7 copy.83
  74.5 1.5 copy.88
  76.1 1.7 copy.85
  77.7 2.5 copy.89
  80.3 1.9 copy.87
  82.1 1.3 copy.90
  83.4 107.7 %while.17 = (s32[]{:T(128)}, f32[1,512,512]{2,1,0:T(8,128)S(1)}, f32[1,512]{1,0:T(1,128)S(1)}, f32[1,512]{1,0:T(1,128)S(1)}, f32[8,128,1,512]{3,1,0,2:T(8,128)},...) while((s32[]{:T(128)}, f32[1,512,512]{2,1,0:T(8,128)S(1)}, ...), condition=%wide.region_6.7_spmd.clone, body=%wide.region_0.6_spmd.clone.sunk | while | flops 506255232 | bytes 6142666 | solution.py:150
  85.5 1.2 subtract_exponential_fusion.6
  86.8 1.2 multiply_add_fusion.3
  92.6 2.0 fusion.123
  95.5 1.4 fusion.120
  100.3 1.2 multiply_add_fusion.3
  106.1 2.0 fusion.123
  108.9 1.4 fusion.120
  112.4 1.2 subtract_exponential_fusion.6
  113.8 1.2 multiply_add_fusion.3
  119.5 2.0 fusion.123
  122.4 1.4 fusion.120
  127.2 1.2 multiply_add_fusion.3
  133.0 2.0 fusion.123
  135.8 1.4 fusion.120
  140.7 1.2 multiply_add_fusion.3
  146.5 2.0 fusion.123
  149.3 1.4 fusion.120
  154.1 1.2 multiply_add_fusion.3
  159.9 2.0 fusion.123
  162.8 1.4 fusion.120
  167.6 1.2 multiply_add_fusion.3
  173.4 2.0 fusion.123
  176.2 1.4 fusion.120
  181.1 1.2 multiply_add_fusion.3
  186.8 2.0 fusion.123
  189.7 1.4 fusion.120
  191.1 5.1 %copy.92 = f32[1024,1,512]{2,1,0:T(1,128)} copy(f32[1024,1,512]{2,0,1:T(8,128)} %bitcast.226) | data formatting | bytes 4194304 | tf_op jit(solution)/shard_map/reshape | solution.py:161
  196.2 3.8 %all-to-all-start.3 = ((f32[1024,1,512]{2,1,0:T(1,128)}), f32[1024,1,512]{2,1,0:T(1,128)S(1)}, u32[]{:S(2)}, u32[]{:S(2)}) async-start(f32[1024,1,512]{2,1,0:T(1,128)} %copy.92), calls=%async_computation.3 | async-start | bytes 4194304 | tf_op jit(solution)/shard_map/all_to_all | solution.py:162
  201.6 24.7 %all-to-all-done.3 = f32[1024,1,512]{2,1,0:T(1,128)S(1)} async-done(((f32[1024,1,512]{2,1,0:T(1,128)}), f32[1024,1,512]{2,1,0:T(1,128)S(1)}, u32[]{:S(2)}, u32[]{:S(2)}) %all-to-all-start.3) | async-done | bytes 2097184 | tf_op jit(solution)/shard_map/all_to_all | solution.py:162
  228.4 1.4 convolution_convert_fusion
  229.8 1.6 fusion.56
  231.4 1.9 copy-done
  233.3 1.3 fusion.88
  235.2 1.2 collective-permute-start.2
  238.1 9.2 %collective-permute-done = bf16[1,64,4096]{2,1,0:T(8,128)(2,1)} collective-permute-done((bf16[1,64,4096]{2,1,0:T(8,128)(2,1)}, bf16[1,64,4096]{2,1,0:T(8,128)(2,1)}, u32[]{:S(2)}, u32[]{:S(2)}) %collective-permute-start) | collective-permute-done | bytes 524320 | tf_op jit(solution)/shard_map/ppermute | solution.py:98
  248.3 10.2 %collective-permute-done.1 = bf16[1,64,4096]{2,1,0:T(8,128)(2,1)} collective-permute-done((bf16[1,64,4096]{2,1,0:T(8,128)(2,1)}, bf16[1,64,4096]{2,1,0:T(8,128)(2,1)}, u32[]{:S(2)}, u32[]{:S(2)}) %collective-permute-start.1) | collective-permute-done | bytes 524320 | tf_op jit(solution)/shard_map/ppermute | solution.py:98
  260.5 21.7 %collective-permute-done.3 = bf16[1,64,4096]{2,1,0:T(8,128)(2,1)S(1)} collective-permute-done((bf16[1,64,4096]{2,1,0:T(8,128)(2,1)S(1)}, bf16[1,64,4096]{2,1,0:T(8,128)(2,1)S(1)}, u32[]{:S(2)}, u32[]{:S(2)}) %collective-permute-start.3) | collective-permute-done | bytes 524320 | tf_op jit(solution)/shard_map/ppermute | solution.py:98
  282.2 1.6 collective-permute-done.4
  283.9 1.2 slice_dynamic-update-slice_fusion
  285.2 1.6 fusion.55
  286.8 2.0 copy-done.1
  288.8 3.2 fusion.50
  291.9 14.1 %convolution_convert_fusion.1 = bf16[512,4096]{1,0:T(8,128)(2,1)} fusion(bf16[1,704,4096]{2,1,0:T(8,128)(2,1)} %param.27, bf16[512,4096]{1,0:T(8,128)(2,1)} %bitcast.222, bf16[1,4096,704]{1,2,0:T(8,128)(2,1)} %param.26, f32[512,704]{0,1:T(8,128)S(1)} %fusion.50), kind=kOutput, calls=%fused_computation.74 | convolution fusion | flops 5909839872 | bytes 21364736 | tf_op jit(solution)/shard_map/dot_general | solution.py:192
  306.0 4.7 %all-to-all-start.4 = ((bf16[8,64,4096]{2,1,0:T(8,128)(2,1)}), bf16[8,64,4096]{2,1,0:T(8,128)(2,1)}, u32[]{:S(2)}, u32[]{:S(2)}) async-start(bf16[8,64,4096]{2,1,0:T(8,128)(2,1)} %bitcast.220), calls=%async_computation.4 | async-start | bytes 8388608 | tf_op jit(solution)/shard_map/all_to_all | solution.py:195
  310.7 49.1 %all-to-all-done.4 = bf16[8,64,4096]{2,1,0:T(8,128)(2,1)} async-done(((bf16[8,64,4096]{2,1,0:T(8,128)(2,1)}), bf16[8,64,4096]{2,1,0:T(8,128)(2,1)}, u32[]{:S(2)}, u32[]{:S(2)}) %all-to-all-start.4) | async-done | bytes 4194336 | tf_op jit(solution)/shard_map/all_to_all | solution.py:195
  359.8 2.9 convolution_multiply_fusion.3
  362.7 4.3 %fusion.54 = bf16[128,4096]{1,0:T(8,128)(2,1)} fusion(f32[128,4096]{1,0:T(8,128)S(1)} %convolution_multiply_fusion.3, bf16[512,4096]{1,0:T(8,128)(2,1)} %bitcast.24, bf16[128,4096]{1,0:T(8,128)(2,1)S(1)} %get-tuple-element.170, f32[128]{0:T(128)S(1)} %get-tuple-element.182, s32[128]{0:T(128)S(1)} %get-tuple-element.185), kind=kOutput, calls=%fused_computation.84 | convolution fusion | flops 539557888 | bytes 8389632 | tf_op jit(solution)/shard_map/dot_general | solution.py:200
  (184 shorter events, 77.0 us)
Async XLA Ops:
  0.0 7.6 %copy-start.3 = (bf16[128,4096]{1,0:T(8,128)(2,1)S(1)}, bf16[128,4096]{1,0:T(8,128)(2,1)}, u32[]{:S(2)}) copy-start(bf16[128,4096]{1,0:T(8,128)(2,1)} %param.19) | copy-start | bytes 3145732
  2.3 20.6 %all-to-all-start = ((bf16[128,8,512]{0,2,1:T(8,128)(2,1)}), bf16[128,8,512]{0,2,1:T(8,128)(2,1)S(1)}, u32[]{:S(2)}, u32[]{:S(2)}) async-start(bf16[128,8,512]{0,2,1:T(8,128)(2,1)} %bitcast.2), calls=%async_computation | async-start | bytes 2097152 | tf_op jit(solution)/shard_map/all_to_all | solution.py:118
  7.6 38.5 %copy-start.7 = (f32[8,128]{1,0:T(8,128)S(1)}, f32[8,128]{1,0:T(8,128)}, u32[]{:S(2)}) copy-start(f32[8,128]{1,0:T(8,128)} %param.21) | copy-start | bytes 12292
  7.6 57.0 %copy-start.8 = (f32[8,128]{1,0:T(8,128)S(1)}, f32[8,128]{1,0:T(8,128)}, u32[]{:S(2)}) copy-start(f32[8,128]{1,0:T(8,128)} %param.22) | copy-start | bytes 12292
  22.9 18.9 %all-to-all-start.1 = ((bf16[128,8,512]{0,2,1:T(8,128)(2,1)}), bf16[128,8,512]{0,2,1:T(8,128)(2,1)S(1)}, u32[]{:S(2)}, u32[]{:S(2)}) async-start(bf16[128,8,512]{0,2,1:T(8,128)(2,1)} %bitcast.5), calls=%async_computation.1 | async-start | bytes 2097152 | tf_op jit(solution)/shard_map/all_to_all | solution.py:119
  41.8 38.5 %all-to-all-start.2 = ((bf16[128,8,512]{0,2,1:T(8,128)(2,1)}), bf16[128,8,512]{0,2,1:T(8,128)(2,1)}, u32[]{:S(2)}, u32[]{:S(2)}) async-start(bf16[128,8,512]{0,2,1:T(8,128)(2,1)} %bitcast.8), calls=%async_computation.2 | async-start | bytes 2097152 | tf_op jit(solution)/shard_map/all_to_all | solution.py:117
  191.1 8.9 %copy-start.6 = (s32[128,2]{0,1:T(2,128)S(1)}, s32[128,2]{0,1:T(2,128)}, u32[]{:S(2)}) copy-start(s32[128,2]{0,1:T(2,128)} %param.28) | copy-start | bytes 3076
  196.2 30.2 %all-to-all-start.3 = ((f32[1024,1,512]{2,1,0:T(1,128)}), f32[1024,1,512]{2,1,0:T(1,128)S(1)}, u32[]{:S(2)}, u32[]{:S(2)}) async-start(f32[1024,1,512]{2,1,0:T(1,128)} %copy.92), calls=%async_computation.3 | async-start | bytes 4194304 | tf_op jit(solution)/shard_map/all_to_all | solution.py:162
  226.5 1.2 copy-start.2
  226.5 1.2 copy-start.4
  226.8 1.6 copy-start.5
  231.4 1.9 copy-start
  234.6 12.6 %collective-permute-start = (bf16[1,64,4096]{2,1,0:T(8,128)(2,1)}, bf16[1,64,4096]{2,1,0:T(8,128)(2,1)}, u32[]{:S(2)}, u32[]{:S(2)}) collective-permute-start(bf16[1,64,4096]{2,1,0:T(8,128)(2,1)} %get-tuple-element.181), channel_id=1, source_target_pairs={{0,28},{4,0},{8,4},{12,8},{16,12},{20,16},{24,20},{28,24},{1,29},{... | collective-permute-start | bytes 1572872 | tf_op jit(solution)/shard_map/ppermute | solution.py:98
  234.7 23.8 %collective-permute-start.1 = (bf16[1,64,4096]{2,1,0:T(8,128)(2,1)}, bf16[1,64,4096]{2,1,0:T(8,128)(2,1)}, u32[]{:S(2)}, u32[]{:S(2)}) collective-permute-start(bf16[1,64,4096]{2,1,0:T(8,128)(2,1)} %get-tuple-element.180), channel_id=1, source_target_pairs={{0,24},{4,28},{8,0},{12,4},{16,8},{20,12},{24,16},{28,20},{1,25},{... | collective-permute-start | bytes 1572872 | tf_op jit(solution)/shard_map/ppermute | solution.py:98
  235.2 25.2 %collective-permute-start.2 = (bf16[1,64,4096]{2,1,0:T(8,128)(2,1)}, bf16[1,64,4096]{2,1,0:T(8,128)(2,1)S(1)}, u32[]{:S(2)}, u32[]{:S(2)}) collective-permute-start(bf16[1,64,4096]{2,1,0:T(8,128)(2,1)} %get-tuple-element.179), channel_id=1, source_target_pairs={{0,20},{4,24},{8,28},{12,0},{16,4},{20,8},{24,12},{28,16},{1,21},{... | collective-permute-start | bytes 1572872 | tf_op jit(solution)/shard_map/ppermute | solution.py:98
  236.4 45.7 %collective-permute-start.3 = (bf16[1,64,4096]{2,1,0:T(8,128)(2,1)S(1)}, bf16[1,64,4096]{2,1,0:T(8,128)(2,1)S(1)}, u32[]{:S(2)}, u32[]{:S(2)}) collective-permute-start(bf16[1,64,4096]{2,1,0:T(8,128)(2,1)S(1)} %get-tuple-element.178), channel_id=1, source_target_pairs={{0,16},{4,20},{8,24},{12,28},{16,0},{20,4},{24,8},{28,12},{1,17},{... | collective-permute-start | bytes 1572872 | tf_op jit(solution)/shard_map/ppermute | solution.py:98
  237.1 46.7 %collective-permute-start.4 = (bf16[1,64,4096]{2,1,0:T(8,128)(2,1)S(1)}, bf16[1,64,4096]{2,1,0:T(8,128)(2,1)S(1)}, u32[]{:S(2)}, u32[]{:S(2)}) collective-permute-start(bf16[1,64,4096]{2,1,0:T(8,128)(2,1)S(1)} %get-tuple-element.177), channel_id=1, source_target_pairs={{0,12},{4,16},{8,20},{12,24},{16,28},{20,0},{24,4},{28,8},{1,13},{... | collective-permute-start | bytes 1572872 | tf_op jit(solution)/shard_map/ppermute | solution.py:98
  247.2 36.6 %collective-permute-start.5 = (bf16[1,64,4096]{2,1,0:T(8,128)(2,1)S(1)}, bf16[1,64,4096]{2,1,0:T(8,128)(2,1)S(1)}, u32[]{:S(2)}, u32[]{:S(2)}) collective-permute-start(bf16[1,64,4096]{2,1,0:T(8,128)(2,1)S(1)} %get-tuple-element.176), channel_id=1, source_target_pairs={{0,8},{4,12},{8,16},{12,20},{16,24},{20,28},{24,0},{28,4},{1,9},{5... | collective-permute-start | bytes 1572872 | tf_op jit(solution)/shard_map/ppermute | solution.py:98
  258.5 25.4 %collective-permute-start.6 = (bf16[1,64,4096]{2,1,0:T(8,128)(2,1)S(1)}, bf16[1,64,4096]{2,1,0:T(8,128)(2,1)S(1)}, u32[]{:S(2)}, u32[]{:S(2)}) collective-permute-start(bf16[1,64,4096]{2,1,0:T(8,128)(2,1)S(1)} %get-tuple-element.175), channel_id=1, source_target_pairs={{0,4},{4,8},{8,12},{12,16},{16,20},{20,24},{24,28},{28,0},{1,5},{5... | collective-permute-start | bytes 1572872 | tf_op jit(solution)/shard_map/ppermute | solution.py:98
  283.9 4.9 %slice-start = ((s8[5767168]{0:T(1024)(128)(4,1)}), s8[4194304]{0:T(1024)(128)(4,1)S(1)}, s32[]{:S(2)}) async-start(s8[5767168]{0:T(1024)(128)(4,1)} %bitcast.232), calls=%async_computation.5 | async-start | bytes 8388608
  285.2 3.6 slice-start.1
  286.8 2.0 copy-start.1
  306.0 4.7 %copy-start.9 = (f32[128,2]{0,1:T(2,128)S(1)}, f32[128,2]{0,1:T(2,128)}, u32[]{:S(2)}) copy-start(f32[128,2]{0,1:T(2,128)} %param.29) | copy-start | bytes 3076
  306.0 53.8 %all-to-all-start.4 = ((bf16[8,64,4096]{2,1,0:T(8,128)(2,1)}), bf16[8,64,4096]{2,1,0:T(8,128)(2,1)}, u32[]{:S(2)}, u32[]{:S(2)}) async-start(bf16[8,64,4096]{2,1,0:T(8,128)(2,1)} %bitcast.220), calls=%async_computation.4 | async-start | bytes 8388608 | tf_op jit(solution)/shard_map/all_to_all | solution.py:195
